TPU v7x, 32 devices: a whole 2x2x4 slice. The times are simulated.
32 devices in a mesh: north: 8 (over y, x, core), deep: 4 (over z).
Axes of the slice: x: 2, y: 2, z: 4, core: 2. Of those that a mesh axis runs over, the one named last changes fastest.
Arguments:
- forcing: float32 [2, 128, 128, 256], P(None, None, 'north', 'deep'), may hold values from -6 to 6
- symbol_x: float32 [128], replicated, may hold values from 0.3 to 3
- symbol_y: float32 [128], replicated, may hold values from 0.3 to 3
- symbol_z: float32 [256], replicated, may hold values from 0.3 to 3
Outputs:
- coefficients: float32 [2, 128, 128, 256], P(None, 'north', 'deep')
All inputs are finite; a program needn't handle non-finite values.
Results may differ from a plain program's by a relative error of at most 0.000084.
Values sent between devices are 32-bit elements; how exact they have to be, the bound alone decides.
A program may use at most 64 MiB of HBM per device.

v0:
```python
import functools
import math

import jax
import jax.numpy as jnp
import numpy as np
from jax import lax
from jax.experimental import pallas as pl
from jax.experimental.pallas import tpu as pltpu
from jax.sharding import PartitionSpec as P

CHUNKS = (1, 1, 2, 4, 4, 3, 1)
EARLY = 2


def transform_table(count):
    rank = np.arange(count)
    odd = (2 * rank[:, None] + 1) * (2 * rank[None, :] + 1) % (8 * count)
    return (np.cos(np.pi / (4 * count) * odd) * np.sqrt(2.0 / count)).astype(np.float32)


def chunk_starts(share):
    unit = max(1, share // sum(CHUNKS))
    found, start = [], 0
    for weight in CHUNKS:
        size = min(unit * weight, share - start)
        if size > 0:
            found.append((start, size))
        start += size
    if start < share:
        found.append((start, share - start))
    return tuple(found)


def halves(values):
    high = values.astype(jnp.bfloat16)
    low = (values - high.astype(jnp.float32)).astype(jnp.bfloat16)
    return high, low


def table_halves(table):
    high = table.astype(jnp.bfloat16)
    low = (table - high.astype(np.float32)).astype(jnp.bfloat16)
    return high, low


def partners(me, count):
    found = []
    for step in range(count - 1, 0, -1):
        if count & (count - 1):
            found.append(lax.rem(me + step, count))
            continue
        other = me
        for bit in range(count.bit_length() - 1):
            if step >> bit & 1:
                other = other + (1 - 2 * ((me // 2**bit) % 2)) * 2**bit
        found.append(other)
    return found


def kernel(
    sizes, forcing, tx, ty, tz, gx, gy, gz, out, symbols, xin, hx, hy, hz, wa, u, v, r, fac,
    in_sem, table_sem, ns_sem, nr_sem, ds_sem, dr_sem,
):
    north, deep, chunks, early = sizes
    fields, share_y, share_z, grid_x = forcing.shape
    share_x, part_y = out.shape[1], out.shape[2]
    grid_y, grid_z = v.shape[1], out.shape[3]
    lanes = fields * share_z
    n, d = lax.axis_index("north"), lax.axis_index("deep")
    norths, deeps = partners(n, north), partners(d, deep)
    deeps = deeps[1:] + deeps[:1]

    barrier = pltpu.get_barrier_semaphore()
    for other in deeps:
        pl.semaphore_signal(barrier, device_id={"deep": other}, device_id_type=pl.DeviceIdType.MESH)
    for other in norths:
        pl.semaphore_signal(barrier, device_id={"north": other}, device_id_type=pl.DeviceIdType.MESH)

    first = pltpu.make_async_copy(tx, hx, table_sem.at[0])
    first.start()
    groups = in_sem.shape[0]
    per = share_y // groups
    loads = []
    for g in range(groups):
        part = (slice(None), pl.ds(g * per, per))
        loads.append(pltpu.make_async_copy(forcing.at[part], xin.at[part], in_sem.at[g]))
        loads[-1].start()
    tables = [pltpu.make_async_copy(source, target, table_sem.at[k + 1]) for k, (source, target) in enumerate(((ty, hy), (tz, hz)))]
    for table in tables:
        table.start()
    at = 0
    for source in (gx, gy, gz):
        span = pl.ds(at, source.shape[1])
        pltpu.make_async_copy(source, symbols.at[:, span], table_sem.at[3]).start()
        at += source.shape[1]

    pair = 2 if per % 2 == 0 else 1

    def along_x(g, start, count):
        for y in range(g * per, (g + 1) * per, pair):
            high, low = halves(
                jnp.concatenate([xin[f, y + k] for k in range(pair) for f in range(fields)], axis=0)
            )
            modes = lax.dot_general(
                hx[pl.ds(start, count), :],
                jnp.concatenate([high, low, high], axis=1),
                (((1,), (1,)), ((), ())),
                preferred_element_type=jnp.float32,
            )
            for k in range(pair):
                wa[pl.ds(start * share_y + y + k, count, stride=share_y), :] = modes[
                    :, k * lanes : (k + 1) * lanes
                ]

    def rows(c, other):
        start, size = chunks[c]
        at = (start * north + other * size) * share_y
        return pl.ds(pl.multiple_of(at, share_y), size * share_y)

    def north_copy(c, target, source):
        return pltpu.make_async_remote_copy(
            src_ref=wa.at[rows(c, target)],
            dst_ref=u.at[rows(c, source)],
            send_sem=ns_sem.at[0],
            recv_sem=nr_sem.at[c],
            device_id={"north": target},
            device_id_type=pl.DeviceIdType.MESH,
        )

    def north_landed(c):
        every = u.at[pl.ds(0, (north - 1) * chunks[c][1] * share_y)]
        pltpu.make_async_copy(every, every, nr_sem.at[c]).wait()

    def deep_copy(c, target, source):
        return pltpu.make_async_remote_copy(
            src_ref=v.at[pl.ds(*chunks[c]), pl.ds(pl.multiple_of(target * part_y, part_y), part_y)],
            dst_ref=r.at[source, pl.ds(*chunks[c])],
            send_sem=ds_sem.at[0],
            recv_sem=dr_sem.at[c],
            device_id={"deep": target},
            device_id_type=pl.DeviceIdType.MESH,
        )

    def deep_landed(c):
        every = r.at[pl.ds(0, deep - 1), pl.ds(0, chunks[c][1])]
        pltpu.make_async_copy(every, every, dr_sem.at[c]).wait()

    def send_north(picked):
        for c in picked:
            for other in norths:
                north_copy(c, other, n).start()
        for c in picked:
            u[rows(c, n), :] = wa[rows(c, n), :]

    split = sum(size for _, size in chunks[:early]) * north
    first.wait()
    for g in range(groups):
        loads[g].wait()
        along_x(g, 0, split)
    pl.semaphore_wait(barrier, north + deep - 2)
    send_north(range(early))
    if split < grid_x:
        for g in range(groups):
            along_x(g, split, grid_x - split)
        send_north(range(early, len(chunks)))

    pltpu.make_async_copy(symbols, symbols, table_sem.at[3]).wait()
    at_y, at_z = grid_x, grid_x + grid_y
    spot = lax.broadcasted_iota(jnp.int32, (part_y, grid_y), 0) + d * part_y
    along = lax.broadcasted_iota(jnp.int32, (part_y, grid_y), 1)
    column = jnp.sum(jnp.where(spot == along, symbols[:, at_y:at_z], 0.0), axis=1, keepdims=True)
    plane = column + symbols[:, at_z:]
    spot = lax.broadcasted_iota(jnp.int32, (share_x, grid_x), 0) + n * share_x
    along = lax.broadcasted_iota(jnp.int32, (share_x, grid_x), 1)
    column = jnp.sum(jnp.where(spot == along, symbols[:, :at_y], 0.0), axis=1, keepdims=True)
    for i in range(share_x):
        symbol = column[i : i + 1] + plane
        fac[pl.ds(i * part_y, part_y), :] = (1.0 - 0.2 * symbol) / (1.0 + 0.2 * symbol)

    mine = pl.ds(pl.multiple_of(d * part_y, part_y), part_y)
    tables[0].wait()
    for c in range(len(chunks)):
        north_landed(c)
        start, size = chunks[c]
        for i in range(0, size, 2):
            pair = min(2, size - i)
            lines = jnp.concatenate(
                [
                    jnp.concatenate(
                        [
                            u[pl.ds((start * north + s * size + i + k) * share_y, share_y), :]
                            for s in range(north)
                        ],
                        axis=0,
                    )
                    for k in range(pair)
                ],
                axis=1,
            )
            high, low = halves(lines)
            modes = jnp.dot(
                hy[...],
                jnp.concatenate([high, low, high], axis=0),
                preferred_element_type=jnp.float32,
            )
            for k in range(pair):
                v[start + i + k] = modes[:, k * lanes : (k + 1) * lanes]
        for other in deeps:
            deep_copy(c, other, d).start()
        r[d, pl.ds(start, size)] = v[pl.ds(start, size), mine]

    tables[1].wait()
    for c in range(len(chunks)):
        start, size = chunks[c]
        deep_landed(c)
        parts = [r[s, pl.ds(*chunks[c])].reshape(size * part_y, lanes) for s in range(deep)]
        factor = fac[pl.ds(start * part_y, size * part_y), :]
        for f in range(fields):
            lines = jnp.concatenate([p[:, f * share_z : (f + 1) * share_z] for p in parts], axis=1)
            high, low = halves(lines)
            modes = jnp.dot(
                jnp.concatenate([high, low, high], axis=1),
                hz[...],
                preferred_element_type=jnp.float32,
            )
            out[f, pl.ds(*chunks[c])] = (modes * factor).reshape(size, part_y, grid_z)

    sent = wa.at[pl.ds(0, (north - 1) * share_x * share_y)]
    pltpu.make_async_copy(sent, sent, ns_sem.at[0]).wait()
    sent = r.at[pl.ds(0, deep - 1)]
    pltpu.make_async_copy(sent, sent, ds_sem.at[0]).wait()


def local(north, deep, forcing, symbol_x, symbol_y, symbol_z):
    fields, grid_x, share_y, share_z = forcing.shape
    grid_y, grid_z = symbol_y.shape[0], symbol_z.shape[0]
    share_x, part_y = grid_x // north, grid_y // deep
    chunks = chunk_starts(share_x)
    lanes = fields * share_z

    modes = np.arange(grid_x).reshape(north, share_x)
    order = np.concatenate([modes[:, start : start + size].reshape(-1) for start, size in chunks])
    high, low = table_halves(transform_table(grid_x)[order])
    hx = np.concatenate([high, high, low], axis=1)
    high, low = table_halves(transform_table(grid_y))
    hy = np.concatenate([high, high, low], axis=1)
    high, low = table_halves(transform_table(grid_z))
    hz = np.concatenate([high, high, low], axis=0)

    groups = share_y // 4 if share_y % 4 == 0 else 1
    vmem = pl.BlockSpec(memory_space=pltpu.VMEM)
    buffers = [
        pltpu.VMEM((fields, share_y, share_z, grid_x), jnp.float32),
        pltpu.VMEM(hx.shape, jnp.bfloat16),
        pltpu.VMEM(hy.shape, jnp.bfloat16),
        pltpu.VMEM(hz.shape, jnp.bfloat16),
        pltpu.VMEM((grid_x * share_y, lanes), jnp.float32),
        pltpu.VMEM((grid_y * share_x, lanes), jnp.float32),
        pltpu.VMEM((share_x, grid_y, lanes), jnp.float32),
        pltpu.VMEM((deep, share_x, part_y, lanes), jnp.float32),
        pltpu.VMEM((share_x * part_y, grid_z), jnp.float32),
    ]
    result = fields * share_x * part_y * grid_z
    held = sum(math.prod(b.shape) * jnp.dtype(b.dtype).itemsize for b in buffers)
    return pl.pallas_call(
        functools.partial(kernel, (north, deep, chunks, min(EARLY, len(chunks)))),
        out_shape=pltpu.VMEM((fields, share_x, part_y, grid_z), jnp.float32),
        in_specs=[pl.BlockSpec(memory_space=pltpu.HBM)] * 7,
        out_specs=vmem,
        scratch_shapes=[
            pltpu.VMEM((1, grid_x + grid_y + grid_z), jnp.float32),
            *buffers,
            pltpu.SemaphoreType.DMA((groups,)),
            pltpu.SemaphoreType.DMA((4,)),
            pltpu.SemaphoreType.DMA((1,)),
            pltpu.SemaphoreType.DMA((len(chunks),)),
            pltpu.SemaphoreType.DMA((1,)),
            pltpu.SemaphoreType.DMA((len(chunks),)),
        ],
        compiler_params=pltpu.CompilerParams(
            collective_id=0, has_side_effects=True, vmem_limit_bytes=max(held + 2**23, 60 * 2**20 - 4 * result)
        ),
    )(
        forcing.transpose(0, 2, 3, 1),
        jnp.asarray(hx),
        jnp.asarray(hy),
        jnp.asarray(hz),
        symbol_x[None, :],
        symbol_y[None, :],
        symbol_z[None, :],
    )


def solution(mesh):
    placed = (P(None, None, "north", "deep"), P(), P(), P())
    return jax.shard_map(
        functools.partial(local, mesh.shape["north"], mesh.shape["deep"]),
        mesh=mesh,
        in_specs=placed,
        out_specs=P(None, "north", "deep", None),
        check_vma=False,
    )
```

profile of v0, /device:TPU:0, one launch (start us, length us, event | category | flops | bytes accessed | tf_op | source)
XLA Modules:
  0.0 35.2 jit_solution(46909775689423296)
XLA Ops:
  0.0 34.3 %shard_map.73 = f32[2,16,32,256]{3,2,1,0:T(8,128)S(1)} custom-call(f32[2,16,64,128]{3,2,1,0:T(8,128)} %bitcast.4, bf16[128,384]{1,0:T(8,128)(2,1)} %constant.6.clone.tx, bf16[128,384]{1,0:T(8,128)(2,1)} %constant.7.clone.ty, bf16[768,256]{1,0:T(8,128)(2,1)} %constant.8.clone.tz, f32[1,128]{1,0:T(1,128)} %bitcast.6, f32[1,128]{1,0:T(1,128)} %bitcast.7, ...), custom_call_target="tpu_custom_call" | custom-call | tf_op jit(solution)/shard_map/pallas_call | solution.py:266
  34.3 1.0 %copy.9 = f32[2,16,32,256]{3,2,1,0:T(8,128)} copy(f32[2,16,32,256]{3,2,1,0:T(8,128)S(1)} %shard_map.73) | data formatting | bytes 2097152
where the time goes:
time: 35.4 us; the launch traced here: 35.2 us
  Pallas kernels  34.3 us (97%)
  local copies, waits for them, and re-layouts  0.97 us (3%)
    pallas_call x1, Pallas kernels, local(): pl.pallas_call(functools.partial(kernel, (north, deep, chunks, min(EARLY,...  34.3 us
    unnamed x1, local copies, waits for them, and re-layouts  0.97 us

commit v1 on v0

--- a/solution.py
+++ b/solution.py
@@ -11,6 +11,7 @@
 
 CHUNKS = (1, 1, 2, 4, 4, 3, 1)
 EARLY = 2
+HELD = 3
 
 
 def transform_table(count):
@@ -69,10 +70,14 @@
     lanes = fields * share_z
     n, d = lax.axis_index("north"), lax.axis_index("deep")
     norths, deeps = partners(n, north), partners(d, deep)
-    deeps = deeps[1:] + deeps[:1]
+    held = ()
+    if deep == 4:
+        far = jnp.where(d < 2, 3, 0)
+        near, side = far + 1 - 2 * (far % 2), d + 1 - 2 * (d % 2)
+        deeps, held = (far, side), (near,)
 
     barrier = pltpu.get_barrier_semaphore()
-    for other in deeps:
+    for other in (*deeps, *held):
         pl.semaphore_signal(barrier, device_id={"deep": other}, device_id_type=pl.DeviceIdType.MESH)
     for other in norths:
         pl.semaphore_signal(barrier, device_id={"north": other}, device_id_type=pl.DeviceIdType.MESH)
@@ -178,6 +183,7 @@
         symbol = column[i : i + 1] + plane
         fac[pl.ds(i * part_y, part_y), :] = (1.0 - 0.2 * symbol) / (1.0 + 0.2 * symbol)
 
+    free = max(0, len(chunks) - HELD)
     mine = pl.ds(pl.multiple_of(d * part_y, part_y), part_y)
     tables[0].wait()
     for c in range(len(chunks)):
@@ -206,8 +212,12 @@
             )
             for k in range(pair):
                 v[start + i + k] = modes[:, k * lanes : (k + 1) * lanes]
-        for other in deeps:
+        last = c == len(chunks) - 1
+        for other in deeps if c >= free else (*deeps[:1], *held, *deeps[1:]):
             deep_copy(c, other, d).start()
+        for late in range(free, len(chunks)) if last else ():
+            for other in held:
+                deep_copy(late, other, d).start()
         r[d, pl.ds(start, size)] = v[pl.ds(start, size), mine]
 
     tables[1].wait()

time: 35.4 us -> 33.1 us (0.935)
  the two profiles are of different devices: /device:TPU:0 before, /device:TPU:8 now
where the time goes in v1:
time: 33.1 us; the launch traced here: 33 us
  Pallas kernels  32 us (97%)
  local copies, waits for them, and re-layouts  0.97 us (3%)
    pallas_call x1, Pallas kernels, local(): pl.pallas_call(functools.partial(kernel, (north, deep, chunks, min(EARLY,...  32 us
    unnamed x1, local copies, waits for them, and re-layouts  0.97 us

profile of v1, /device:TPU:8, one launch (start us, length us, event | category | flops | bytes accessed | tf_op | source)
XLA Modules:
  0.0 33.0 jit_solution(6779763874165109021)
XLA Ops:
  0.0 32.0 %shard_map.73 = f32[2,16,32,256]{3,2,1,0:T(8,128)S(1)} custom-call(f32[2,16,64,128]{3,2,1,0:T(8,128)} %bitcast.4, bf16[128,384]{1,0:T(8,128)(2,1)} %constant.6.clone.tx, bf16[128,384]{1,0:T(8,128)(2,1)} %constant.7.clone.ty, bf16[768,256]{1,0:T(8,128)(2,1)} %constant.8.clone.tz, f32[1,128]{1,0:T(1,128)} %bitcast.6, f32[1,128]{1,0:T(1,128)} %bitcast.7, ...), custom_call_target="tpu_custom_call" | custom-call | tf_op jit(solution)/shard_map/pallas_call | solution.py:276
  32.0 1.0 %copy.9 = f32[2,16,32,256]{3,2,1,0:T(8,128)} copy(f32[2,16,32,256]{3,2,1,0:T(8,128)S(1)} %shard_map.73) | data formatting | bytes 2097152

commit v2 on v1

--- a/solution.py
+++ b/solution.py
@@ -9,9 +9,11 @@
 from jax.experimental.pallas import tpu as pltpu
 from jax.sharding import PartitionSpec as P
 
-CHUNKS = (1, 1, 2, 4, 4, 3, 1)
+CHUNKS = (1, 2, 1, 4, 4, 3, 1)
 EARLY = 2
 HELD = 3
+AHEAD = 1
+RELAY = 3
 
 
 def transform_table(count):
@@ -60,14 +62,15 @@
 
 
 def kernel(
-    sizes, forcing, tx, ty, tz, gx, gy, gz, out, symbols, xin, hx, hy, hz, wa, u, v, r, fac,
-    in_sem, table_sem, ns_sem, nr_sem, ds_sem, dr_sem,
+    sizes, forcing, tx, ty, tz, gx, gy, gz, out, symbols, xin, hx, hy, hz, wa, u, v, r, fac, ein, eu, ev,
+    in_sem, table_sem, ns_sem, nr_sem, ds_sem, dr_sem, round_sem, ahead_sem,
 ):
     north, deep, chunks, early = sizes
     fields, share_y, share_z, grid_x = forcing.shape
     share_x, part_y = out.shape[1], out.shape[2]
     grid_y, grid_z = v.shape[1], out.shape[3]
-    lanes = fields * share_z
+    lanes, rounds = fields * share_z, max(0, deep - 2)
+    ahead = deep == 4 and len(chunks) > RELAY
     n, d = lax.axis_index("north"), lax.axis_index("deep")
     norths, deeps = partners(n, north), partners(d, deep)
     held = ()
@@ -77,8 +80,17 @@
         deeps, held = (far, side), (near,)
 
     barrier = pltpu.get_barrier_semaphore()
-    for other in (*deeps, *held):
-        pl.semaphore_signal(barrier, device_id={"deep": other}, device_id_type=pl.DeviceIdType.MESH)
+    inner = (d > 0).astype(jnp.int32) + (d < deep - 1).astype(jnp.int32)
+
+    def signal_beside(semaphore):
+        for other, there in ((d - 1, d > 0), (d + 1, d < deep - 1)):
+            @pl.when(there)
+            def _():
+                pl.semaphore_signal(
+                    semaphore, device_id={"deep": other}, device_id_type=pl.DeviceIdType.MESH
+                )
+
+    signal_beside(barrier)
     for other in norths:
         pl.semaphore_signal(barrier, device_id={"north": other}, device_id_type=pl.DeviceIdType.MESH)
 
@@ -92,14 +104,6 @@
         loads.append(pltpu.make_async_copy(forcing.at[part], xin.at[part], in_sem.at[g]))
         loads[-1].start()
     tables = [pltpu.make_async_copy(source, target, table_sem.at[k + 1]) for k, (source, target) in enumerate(((ty, hy), (tz, hz)))]
-    for table in tables:
-        table.start()
-    at = 0
-    for source in (gx, gy, gz):
-        span = pl.ds(at, source.shape[1])
-        pltpu.make_async_copy(source, symbols.at[:, span], table_sem.at[3]).start()
-        at += source.shape[1]
-
     pair = 2 if per % 2 == 0 else 1
 
     def along_x(g, start, count):
@@ -107,12 +111,13 @@
             high, low = halves(
                 jnp.concatenate([xin[f, y + k] for k in range(pair) for f in range(fields)], axis=0)
             )
-            modes = lax.dot_general(
-                hx[pl.ds(start, count), :],
-                jnp.concatenate([high, low, high], axis=1),
+            both = lax.dot_general(
+                hx[pl.ds(2 * start, 2 * count), :],
+                jnp.concatenate([high, low], axis=1),
                 (((1,), (1,)), ((), ())),
                 preferred_element_type=jnp.float32,
             )
+            modes = both[:count] + both[count:]
             for k in range(pair):
                 wa[pl.ds(start * share_y + y + k, count, stride=share_y), :] = modes[
                     :, k * lanes : (k + 1) * lanes
@@ -148,8 +153,50 @@
         )
 
     def deep_landed(c):
-        every = r.at[pl.ds(0, deep - 1), pl.ds(0, chunks[c][1])]
-        pltpu.make_async_copy(every, every, dr_sem.at[c]).wait()
+        def take(count):
+            every = r.at[pl.ds(0, count), pl.ds(0, chunks[c][1])]
+            pltpu.make_async_copy(every, every, dr_sem.at[c]).wait()
+
+        if ahead and c == AHEAD:
+            pl.when(d == 1)(lambda: take(deep - 2))
+            pl.when(d != 1)(lambda: take(deep - 1))
+        else:
+            take(deep - 1)
+
+    def ahead_rows(other, count=1):
+        size = chunks[AHEAD][1] * share_y
+        return pl.ds(pl.multiple_of(other * size, size), count * size)
+
+    def ahead_down():
+        start, size = chunks[AHEAD]
+        return pltpu.make_async_remote_copy(
+            src_ref=wa.at[pl.ds(start * north * share_y, size * north * share_y)],
+            dst_ref=ein,
+            send_sem=ahead_sem.at[0],
+            recv_sem=ahead_sem.at[1],
+            device_id={"deep": 1},
+            device_id_type=pl.DeviceIdType.MESH,
+        )
+
+    def ahead_across(target, source):
+        return pltpu.make_async_remote_copy(
+            src_ref=ein.at[ahead_rows(target)],
+            dst_ref=eu.at[ahead_rows(source)],
+            send_sem=ahead_sem.at[2],
+            recv_sem=ahead_sem.at[3],
+            device_id={"north": target},
+            device_id_type=pl.DeviceIdType.MESH,
+        )
+
+    def ahead_on():
+        return pltpu.make_async_remote_copy(
+            src_ref=ev.at[:, pl.ds(0, part_y)],
+            dst_ref=r.at[2, pl.ds(*chunks[AHEAD])],
+            send_sem=ahead_sem.at[4],
+            recv_sem=dr_sem.at[AHEAD],
+            device_id={"deep": 0},
+            device_id_type=pl.DeviceIdType.MESH,
+        )
 
     def send_north(picked):
         for c in picked:
@@ -162,14 +209,29 @@
     first.wait()
     for g in range(groups):
         loads[g].wait()
+    for g in range(groups):
         along_x(g, 0, split)
-    pl.semaphore_wait(barrier, north + deep - 2)
+    for table in tables:
+        table.start()
+    at = 0
+    for source in (gx, gy, gz):
+        span = pl.ds(at, source.shape[1])
+        pltpu.make_async_copy(source, symbols.at[:, span], table_sem.at[3]).start()
+        at += source.shape[1]
+    pl.semaphore_wait(barrier, north - 1 + inner)
+    if ahead:
+        pl.when(d == 2)(lambda: ahead_down().start())
     send_north(range(early))
+    if rounds:
+        signal_beside(round_sem.at[0])
     if split < grid_x:
         for g in range(groups):
             along_x(g, split, grid_x - split)
         send_north(range(early, len(chunks)))
 
+    for k in range(rounds - 1):
+        pl.semaphore_wait(round_sem.at[k], inner)
+        signal_beside(round_sem.at[k + 1])
     pltpu.make_async_copy(symbols, symbols, table_sem.at[3]).wait()
     at_y, at_z = grid_x, grid_x + grid_y
     spot = lax.broadcasted_iota(jnp.int32, (part_y, grid_y), 0) + d * part_y
@@ -183,42 +245,73 @@
         symbol = column[i : i + 1] + plane
         fac[pl.ds(i * part_y, part_y), :] = (1.0 - 0.2 * symbol) / (1.0 + 0.2 * symbol)
 
+    def along_y(blocks, base, size, i, pair, count):
+        lines = jnp.concatenate(
+            [
+                jnp.concatenate(
+                    [blocks[pl.ds(base + (s * size + i + k) * share_y, share_y), :] for s in range(north)],
+                    axis=0,
+                )
+                for k in range(pair)
+            ],
+            axis=1,
+        )
+        high, low = halves(lines)
+        return jnp.dot(
+            hy[pl.ds(0, count), :],
+            jnp.concatenate([high, low, high], axis=0),
+            preferred_element_type=jnp.float32,
+        )
+
     free = max(0, len(chunks) - HELD)
     mine = pl.ds(pl.multiple_of(d * part_y, part_y), part_y)
     tables[0].wait()
     for c in range(len(chunks)):
         north_landed(c)
+        if c == 0 and rounds:
+            pl.semaphore_wait(round_sem.at[rounds - 1], inner)
         start, size = chunks[c]
         for i in range(0, size, 2):
             pair = min(2, size - i)
-            lines = jnp.concatenate(
-                [
-                    jnp.concatenate(
-                        [
-                            u[pl.ds((start * north + s * size + i + k) * share_y, share_y), :]
-                            for s in range(north)
-                        ],
-                        axis=0,
-                    )
-                    for k in range(pair)
-                ],
-                axis=1,
-            )
-            high, low = halves(lines)
-            modes = jnp.dot(
-                hy[...],
-                jnp.concatenate([high, low, high], axis=0),
-                preferred_element_type=jnp.float32,
-            )
+            modes = along_y(u, start * north * share_y, size, i, pair, grid_y)
             for k in range(pair):
                 v[start + i + k] = modes[:, k * lanes : (k + 1) * lanes]
         last = c == len(chunks) - 1
-        for other in deeps if c >= free else (*deeps[:1], *held, *deeps[1:]):
-            deep_copy(c, other, d).start()
+        if ahead and c == AHEAD:
+            @pl.when(d != 2)
+            def _():
+                for other in (deeps[0], *held):
+                    deep_copy(c, other, d).start()
+
+            deep_copy(c, deeps[1], d).start()
+        else:
+            for other in deeps if c >= free else (*deeps[:1], *held, *deeps[1:]):
+                deep_copy(c, other, d).start()
         for late in range(free, len(chunks)) if last else ():
             for other in held:
                 deep_copy(late, other, d).start()
         r[d, pl.ds(start, size)] = v[pl.ds(start, size), mine]
+        if ahead and c == RELAY:
+            @pl.when(d == 1)
+            def _():
+                ahead_down().wait_recv()
+                for other in norths:
+                    ahead_across(other, n).start()
+                eu[ahead_rows(n), :] = ein[ahead_rows(n), :]
+
+    if ahead:
+        @pl.when(d == 1)
+        def _():
+            start, size = chunks[AHEAD]
+            every = eu.at[ahead_rows(0, north - 1)]
+            pltpu.make_async_copy(every, every, ahead_sem.at[3]).wait()
+            for i in range(0, size, 2):
+                pair = min(2, size - i)
+                modes = along_y(eu, 0, size, i, pair, 2 * part_y)
+                for k in range(pair):
+                    ev[i + k] = modes[:, k * lanes : (k + 1) * lanes]
+            ahead_on().start()
+            r[2, pl.ds(start, size)] = ev[:, part_y:]
 
     tables[1].wait()
     for c in range(len(chunks)):
@@ -238,8 +331,26 @@
 
     sent = wa.at[pl.ds(0, (north - 1) * share_x * share_y)]
     pltpu.make_async_copy(sent, sent, ns_sem.at[0]).wait()
-    sent = r.at[pl.ds(0, deep - 1)]
-    pltpu.make_async_copy(sent, sent, ds_sem.at[0]).wait()
+    every = r.at[pl.ds(0, deep - 1)]
+    if ahead:
+        @pl.when(d == 2)
+        def _():
+            rest = share_x * (deep - 1) - 2 * chunks[AHEAD][1]
+            some = wa.at[pl.ds(0, rest * part_y)]
+            pltpu.make_async_copy(some, some, ds_sem.at[0]).wait()
+            ahead_down().wait_send()
+
+        @pl.when(d != 2)
+        def _():
+            pltpu.make_async_copy(every, every, ds_sem.at[0]).wait()
+
+        @pl.when(d == 1)
+        def _():
+            sent = ein.at[ahead_rows(0, north - 1)]
+            pltpu.make_async_copy(sent, sent, ahead_sem.at[2]).wait()
+            ahead_on().wait_send()
+    else:
+        pltpu.make_async_copy(every, every, ds_sem.at[0]).wait()
 
 
 def local(north, deep, forcing, symbol_x, symbol_y, symbol_z):
@@ -252,13 +363,20 @@
     modes = np.arange(grid_x).reshape(north, share_x)
     order = np.concatenate([modes[:, start : start + size].reshape(-1) for start, size in chunks])
     high, low = table_halves(transform_table(grid_x)[order])
-    hx = np.concatenate([high, high, low], axis=1)
+    split = sum(size for _, size in chunks[:EARLY]) * north
+    hx = np.concatenate(
+        [
+            np.block([[high[part], high[part]], [low[part], np.zeros_like(low[part])]])
+            for part in (slice(0, split), slice(split, grid_x))
+        ],
+        axis=0,
+    )
     high, low = table_halves(transform_table(grid_y))
     hy = np.concatenate([high, high, low], axis=1)
     high, low = table_halves(transform_table(grid_z))
     hz = np.concatenate([high, high, low], axis=0)
 
-    groups = share_y // 4 if share_y % 4 == 0 else 1
+    groups, extra = 1, chunks[min(AHEAD, len(chunks) - 1)][1]
     vmem = pl.BlockSpec(memory_space=pltpu.VMEM)
     buffers = [
         pltpu.VMEM((fields, share_y, share_z, grid_x), jnp.float32),
@@ -270,6 +388,9 @@
         pltpu.VMEM((share_x, grid_y, lanes), jnp.float32),
         pltpu.VMEM((deep, share_x, part_y, lanes), jnp.float32),
         pltpu.VMEM((share_x * part_y, grid_z), jnp.float32),
+        pltpu.VMEM((extra * north * share_y, lanes), jnp.float32),
+        pltpu.VMEM((extra * north * share_y, lanes), jnp.float32),
+        pltpu.VMEM((extra, 2 * part_y, lanes), jnp.float32),
     ]
     result = fields * share_x * part_y * grid_z
     held = sum(math.prod(b.shape) * jnp.dtype(b.dtype).itemsize for b in buffers)
@@ -287,6 +408,8 @@
             pltpu.SemaphoreType.DMA((len(chunks),)),
             pltpu.SemaphoreType.DMA((1,)),
             pltpu.SemaphoreType.DMA((len(chunks),)),
+            pltpu.SemaphoreType.REGULAR((max(1, deep - 2),)),
+            pltpu.SemaphoreType.DMA((5,)),
         ],
         compiler_params=pltpu.CompilerParams(
             collective_id=0, has_side_effects=True, vmem_limit_bytes=max(held + 2**23, 60 * 2**20 - 4 * result)

time: 33.1 us -> 32.2 us (0.973)
  Pallas kernels: 32 us -> 31 us
    pallas_call x1, Pallas kernels: 32 us -> 31 us  [local(): pl.pallas_call(functools.partial(kernel, (north, deep, chunks, min(EARLY,...]
where the time goes in v2:
time: 32.2 us; the launch traced here: 32 us
  Pallas kernels  31 us (96%)
  local copies, waits for them, and re-layouts  0.97 us (3%)
    pallas_call x1, Pallas kernels, local(): pl.pallas_call(functools.partial(kernel, (north, deep, chunks, min(EARLY,...  31 us
    unnamed x1, local copies, waits for them, and re-layouts  0.97 us

profile of v2, /device:TPU:8, one launch (start us, length us, event | category | flops | bytes accessed | tf_op | source)
XLA Modules:
  0.0 32.0 jit_solution(14664400254944856693)
XLA Ops:
  0.0 31.0 %shard_map.73 = f32[2,16,32,256]{3,2,1,0:T(8,128)S(1)} custom-call(f32[2,16,64,128]{3,2,1,0:T(8,128)} %bitcast.4, bf16[256,256]{1,0:T(8,128)(2,1)} %constant.6.clone.tx, bf16[128,384]{1,0:T(8,128)(2,1)} %constant.7.clone.ty, bf16[768,256]{1,0:T(8,128)(2,1)} %constant.8.clone.tz, f32[1,128]{1,0:T(1,128)} %bitcast.6, f32[1,128]{1,0:T(1,128)} %bitcast.7, ...), custom_call_target="tpu_custom_call" | custom-call | tf_op jit(solution)/shard_map/pallas_call | solution.py:397
  31.0 1.0 %copy.9 = f32[2,16,32,256]{3,2,1,0:T(8,128)} copy(f32[2,16,32,256]{3,2,1,0:T(8,128)S(1)} %shard_map.73) | data formatting | bytes 2097152

commit v3 on v2

--- a/solution.py
+++ b/solution.py
@@ -14,6 +14,9 @@
 HELD = 3
 AHEAD = 1
 RELAY = 3
+NEAR_NOW = (0, 1, 2, 3)
+NEAR_AFTER = {}
+NEAR_THEN = {3: (4, 5, 6)}
 
 
 def transform_table(count):
@@ -73,11 +76,21 @@
     ahead = deep == 4 and len(chunks) > RELAY
     n, d = lax.axis_index("north"), lax.axis_index("deep")
     norths, deeps = partners(n, north), partners(d, deep)
-    held = ()
+    held, inward = (), (d == 1) | (d == 2)
     if deep == 4:
         far = jnp.where(d < 2, 3, 0)
         near, side = far + 1 - 2 * (far % 2), d + 1 - 2 * (d % 2)
         deeps, held = (far, side), (near,)
+
+    first = pltpu.make_async_copy(tx, hx, table_sem.at[0])
+    groups = in_sem.shape[0]
+    per = share_y // groups
+    loads = []
+    for g in range(groups):
+        part = (slice(None), pl.ds(g * per, per))
+        loads.append(pltpu.make_async_copy(forcing.at[part], xin.at[part], in_sem.at[g]))
+        loads[-1].start()
+    first.start()
 
     barrier = pltpu.get_barrier_semaphore()
     inner = (d > 0).astype(jnp.int32) + (d < deep - 1).astype(jnp.int32)
@@ -93,16 +106,6 @@
     signal_beside(barrier)
     for other in norths:
         pl.semaphore_signal(barrier, device_id={"north": other}, device_id_type=pl.DeviceIdType.MESH)
-
-    first = pltpu.make_async_copy(tx, hx, table_sem.at[0])
-    first.start()
-    groups = in_sem.shape[0]
-    per = share_y // groups
-    loads = []
-    for g in range(groups):
-        part = (slice(None), pl.ds(g * per, per))
-        loads.append(pltpu.make_async_copy(forcing.at[part], xin.at[part], in_sem.at[g]))
-        loads[-1].start()
     tables = [pltpu.make_async_copy(source, target, table_sem.at[k + 1]) for k, (source, target) in enumerate(((ty, hy), (tz, hz)))]
     pair = 2 if per % 2 == 0 else 1
 
@@ -172,8 +175,8 @@
         return pltpu.make_async_remote_copy(
             src_ref=wa.at[pl.ds(start * north * share_y, size * north * share_y)],
             dst_ref=ein,
-            send_sem=ahead_sem.at[0],
-            recv_sem=ahead_sem.at[1],
+            send_sem=ahead_sem.at[2],
+            recv_sem=ahead_sem.at[0],
             device_id={"deep": 1},
             device_id_type=pl.DeviceIdType.MESH,
         )
@@ -183,7 +186,7 @@
             src_ref=ein.at[ahead_rows(target)],
             dst_ref=eu.at[ahead_rows(source)],
             send_sem=ahead_sem.at[2],
-            recv_sem=ahead_sem.at[3],
+            recv_sem=ahead_sem.at[1],
             device_id={"north": target},
             device_id_type=pl.DeviceIdType.MESH,
         )
@@ -192,7 +195,7 @@
         return pltpu.make_async_remote_copy(
             src_ref=ev.at[:, pl.ds(0, part_y)],
             dst_ref=r.at[2, pl.ds(*chunks[AHEAD])],
-            send_sem=ahead_sem.at[4],
+            send_sem=ds_sem.at[0],
             recv_sem=dr_sem.at[AHEAD],
             device_id={"deep": 0},
             device_id_type=pl.DeviceIdType.MESH,
@@ -264,6 +267,29 @@
         )
 
     free = max(0, len(chunks) - HELD)
+    def send_deep(c):
+        if ahead and c == AHEAD:
+            @pl.when(d != 2)
+            def _():
+                for other in (deeps[0], *held):
+                    deep_copy(c, other, d).start()
+
+            deep_copy(c, deeps[1], d).start()
+        elif held:
+            far, side = deeps
+            deep_copy(c, far, d).start()
+            if c < free:
+                if c in NEAR_NOW:
+                    deep_copy(c, held[0], d).start()
+                else:
+                    pl.when(~inward)(lambda: deep_copy(c, held[0], d).start())
+                deep_copy(c, side, d).start()
+            else:
+                pl.when(inward)(lambda: deep_copy(c, side, d).start())
+        else:
+            for other in deeps:
+                deep_copy(c, other, d).start()
+
     mine = pl.ds(pl.multiple_of(d * part_y, part_y), part_y)
     tables[0].wait()
     for c in range(len(chunks)):
@@ -277,19 +303,16 @@
             for k in range(pair):
                 v[start + i + k] = modes[:, k * lanes : (k + 1) * lanes]
         last = c == len(chunks) - 1
-        if ahead and c == AHEAD:
-            @pl.when(d != 2)
+        send_deep(c)
+        if held:
+            for late in NEAR_AFTER.get(c, ()):
+                pl.when(inward)(lambda late=late: deep_copy(late, held[0], d).start())
+        if last and held:
+            @pl.when(~inward)
             def _():
-                for other in (deeps[0], *held):
-                    deep_copy(c, other, d).start()
-
-            deep_copy(c, deeps[1], d).start()
-        else:
-            for other in deeps if c >= free else (*deeps[:1], *held, *deeps[1:]):
-                deep_copy(c, other, d).start()
-        for late in range(free, len(chunks)) if last else ():
-            for other in held:
-                deep_copy(late, other, d).start()
+                for other in (deeps[1], *held):
+                    for late in range(free, len(chunks)):
+                        deep_copy(late, other, d).start()
         r[d, pl.ds(start, size)] = v[pl.ds(start, size), mine]
         if ahead and c == RELAY:
             @pl.when(d == 1)
@@ -304,7 +327,7 @@
         def _():
             start, size = chunks[AHEAD]
             every = eu.at[ahead_rows(0, north - 1)]
-            pltpu.make_async_copy(every, every, ahead_sem.at[3]).wait()
+            pltpu.make_async_copy(every, every, ahead_sem.at[1]).wait()
             for i in range(0, size, 2):
                 pair = min(2, size - i)
                 modes = along_y(eu, 0, size, i, pair, 2 * part_y)
@@ -314,43 +337,71 @@
             r[2, pl.ds(start, size)] = ev[:, part_y:]
 
     tables[1].wait()
-    for c in range(len(chunks)):
+    order = list(range(len(chunks)))
+    if ahead:
+        order.remove(AHEAD)
+        order.insert(free - 1, AHEAD)
+    for c in order:
         start, size = chunks[c]
         deep_landed(c)
+        if held:
+            for late in NEAR_THEN.get(c, ()):
+                pl.when(inward)(lambda late=late: deep_copy(late, held[0], d).start())
         parts = [r[s, pl.ds(*chunks[c])].reshape(size * part_y, lanes) for s in range(deep)]
         factor = fac[pl.ds(start * part_y, size * part_y), :]
-        for f in range(fields):
-            lines = jnp.concatenate([p[:, f * share_z : (f + 1) * share_z] for p in parts], axis=1)
-            high, low = halves(lines)
-            modes = jnp.dot(
-                jnp.concatenate([high, low, high], axis=1),
-                hz[...],
+        lines = [
+            jnp.concatenate([p[:, f * share_z : (f + 1) * share_z] for p in parts], axis=1)
+            for f in range(fields)
+        ]
+        if size == 1:
+            count = fields * size * part_y
+            high, low = halves(jnp.concatenate(lines, axis=0))
+            both = jnp.dot(
+                jnp.concatenate([high, low], axis=0),
+                hz[pl.ds(0, grid_z), :],
                 preferred_element_type=jnp.float32,
             )
-            out[f, pl.ds(*chunks[c])] = (modes * factor).reshape(size, part_y, grid_z)
-
-    sent = wa.at[pl.ds(0, (north - 1) * share_x * share_y)]
-    pltpu.make_async_copy(sent, sent, ns_sem.at[0]).wait()
-    every = r.at[pl.ds(0, deep - 1)]
+            rest = jnp.dot(high, hz[pl.ds(2 * grid_z, grid_z), :], preferred_element_type=jnp.float32)
+            modes = both[:count] + both[count:] + rest
+            modes = [modes[f * size * part_y : (f + 1) * size * part_y] for f in range(fields)]
+        else:
+            modes = []
+            for f in range(fields):
+                high, low = halves(lines[f])
+                modes.append(
+                    jnp.dot(
+                        jnp.concatenate([high, low, high], axis=1),
+                        hz[...],
+                        preferred_element_type=jnp.float32,
+                    )
+                )
+        for f in range(fields):
+            out[f, pl.ds(*chunks[c])] = (modes[f] * factor).reshape(size, part_y, grid_z)
+
+    def sent(semaphore, count):
+        every = wa.at[pl.ds(0, count)]
+        pltpu.make_async_copy(every, every, semaphore).wait()
+
+    across, along = (north - 1) * share_x * share_y, (deep - 1) * share_x * part_y
+    sent(ns_sem.at[0], across)
     if ahead:
+        extra = chunks[AHEAD][1]
+
+        @pl.when(d == 1)
+        def _():
+            sent(ahead_sem.at[2], (north - 1) * extra * share_y)
+            sent(ds_sem.at[0], along + extra * part_y)
+
         @pl.when(d == 2)
         def _():
-            rest = share_x * (deep - 1) - 2 * chunks[AHEAD][1]
-            some = wa.at[pl.ds(0, rest * part_y)]
-            pltpu.make_async_copy(some, some, ds_sem.at[0]).wait()
-            ahead_down().wait_send()
-
-        @pl.when(d != 2)
+            sent(ahead_sem.at[2], north * extra * share_y)
+            sent(ds_sem.at[0], along - 2 * extra * part_y)
+
+        @pl.when((d == 0) | (d == 3))
         def _():
-            pltpu.make_async_copy(every, every, ds_sem.at[0]).wait()
-
-        @pl.when(d == 1)
-        def _():
-            sent = ein.at[ahead_rows(0, north - 1)]
-            pltpu.make_async_copy(sent, sent, ahead_sem.at[2]).wait()
-            ahead_on().wait_send()
+            sent(ds_sem.at[0], along)
     else:
-        pltpu.make_async_copy(every, every, ds_sem.at[0]).wait()
+        sent(ds_sem.at[0], along)
 
 
 def local(north, deep, forcing, symbol_x, symbol_y, symbol_z):
@@ -409,7 +460,7 @@
             pltpu.SemaphoreType.DMA((1,)),
             pltpu.SemaphoreType.DMA((len(chunks),)),
             pltpu.SemaphoreType.REGULAR((max(1, deep - 2),)),
-            pltpu.SemaphoreType.DMA((5,)),
+            pltpu.SemaphoreType.DMA((3,)),
         ],
         compiler_params=pltpu.CompilerParams(
             collective_id=0, has_side_effects=True, vmem_limit_bytes=max(held + 2**23, 60 * 2**20 - 4 * result)

time: 32.2 us -> 32 us (level)
  no operation moved by 1% of the time
where the time goes in v3:
time: 32 us; the launch traced here: 31.8 us
  Pallas kernels  30.9 us (97%)
  local copies, waits for them, and re-layouts  0.97 us (3%)
    pallas_call x1, Pallas kernels, local(): pl.pallas_call(functools.partial(kernel, (north, deep, chunks, min(EARLY,...  30.9 us
    unnamed x1, local copies, waits for them, and re-layouts  0.97 us

profile of v3, /device:TPU:8, one launch (start us, length us, event | category | flops | bytes accessed | tf_op | source)
XLA Modules:
  0.0 31.8 jit_solution(9187124346753193667)
XLA Ops:
  0.0 30.9 %shard_map.73 = f32[2,16,32,256]{3,2,1,0:T(8,128)S(1)} custom-call(f32[2,16,64,128]{3,2,1,0:T(8,128)} %bitcast.4, bf16[256,256]{1,0:T(8,128)(2,1)} %constant.6.clone.tx, bf16[128,384]{1,0:T(8,128)(2,1)} %constant.7.clone.ty, bf16[768,256]{1,0:T(8,128)(2,1)} %constant.8.clone.tz, f32[1,128]{1,0:T(1,128)} %bitcast.6, f32[1,128]{1,0:T(1,128)} %bitcast.7, ...), custom_call_target="tpu_custom_call" | custom-call | tf_op jit(solution)/shard_map/pallas_call | solution.py:448
  30.9 1.0 %copy.9 = f32[2,16,32,256]{3,2,1,0:T(8,128)} copy(f32[2,16,32,256]{3,2,1,0:T(8,128)S(1)} %shard_map.73) | data formatting | bytes 2097152

commit v4 on v3

--- a/solution.py
+++ b/solution.py
@@ -10,9 +10,10 @@
 from jax.sharding import PartitionSpec as P
 
 CHUNKS = (1, 2, 1, 4, 4, 3, 1)
-EARLY = 2
+EARLY = 3
 HELD = 3
 AHEAD = 1
+FEW = 2
 RELAY = 3
 NEAR_NOW = (0, 1, 2, 3)
 NEAR_AFTER = {}
@@ -65,7 +66,7 @@
 
 
 def kernel(
-    sizes, forcing, tx, ty, tz, gx, gy, gz, out, symbols, xin, hx, hy, hz, wa, u, v, r, fac, ein, eu, ev,
+    sizes, forcing, tx, ty, tz, gx, gy, gz, out, final, factors, hz, symbols, xin, hx, hy, wa, u, v, r, fac, ein, eu, ev,
     in_sem, table_sem, ns_sem, nr_sem, ds_sem, dr_sem, round_sem, ahead_sem,
 ):
     north, deep, chunks, early = sizes
@@ -73,10 +74,12 @@
     share_x, part_y = out.shape[1], out.shape[2]
     grid_y, grid_z = v.shape[1], out.shape[3]
     lanes, rounds = fields * share_z, max(0, deep - 2)
-    ahead = deep == 4 and len(chunks) > RELAY
+    few = min(FEW, north)
+    ahead = merged = deep == 4 and len(chunks) > RELAY
     n, d = lax.axis_index("north"), lax.axis_index("deep")
     norths, deeps = partners(n, north), partners(d, deep)
-    held, inward = (), (d == 1) | (d == 2)
+    held, inward, favoured = (), (d == 1) | (d == 2), n < FEW
+    patient = (d == 3) & favoured
     if deep == 4:
         far = jnp.where(d < 2, 3, 0)
         near, side = far + 1 - 2 * (far % 2), d + 1 - 2 * (d % 2)
@@ -126,6 +129,9 @@
                     :, k * lanes : (k + 1) * lanes
                 ]
 
+    def landing(c):
+        return (c or RELAY) - 1 if merged else c
+
     def rows(c, other):
         start, size = chunks[c]
         at = (start * north + other * size) * share_y
@@ -136,13 +142,14 @@
             src_ref=wa.at[rows(c, target)],
             dst_ref=u.at[rows(c, source)],
             send_sem=ns_sem.at[0],
-            recv_sem=nr_sem.at[c],
+            recv_sem=nr_sem.at[min(c, len(chunks) - 2)],
             device_id={"north": target},
             device_id_type=pl.DeviceIdType.MESH,
         )
 
     def north_landed(c):
-        every = u.at[pl.ds(0, (north - 1) * chunks[c][1] * share_y)]
+        size = sum(size for _, size in chunks[c:]) if c == len(chunks) - 2 else chunks[c][1]
+        every = u.at[pl.ds(0, (north - 1) * size * share_y)]
         pltpu.make_async_copy(every, every, nr_sem.at[c]).wait()
 
     def deep_copy(c, target, source):
@@ -150,56 +157,65 @@
             src_ref=v.at[pl.ds(*chunks[c]), pl.ds(pl.multiple_of(target * part_y, part_y), part_y)],
             dst_ref=r.at[source, pl.ds(*chunks[c])],
             send_sem=ds_sem.at[0],
-            recv_sem=dr_sem.at[c],
+            recv_sem=dr_sem.at[landing(c)],
             device_id={"deep": target},
             device_id_type=pl.DeviceIdType.MESH,
         )
 
     def deep_landed(c):
+        size = chunks[c][1] + (chunks[0][1] if merged and c == RELAY else 0)
+
         def take(count):
-            every = r.at[pl.ds(0, count), pl.ds(0, chunks[c][1])]
-            pltpu.make_async_copy(every, every, dr_sem.at[c]).wait()
-
-        if ahead and c == AHEAD:
-            pl.when(d == 1)(lambda: take(deep - 2))
-            pl.when(d != 1)(lambda: take(deep - 1))
+            every = r.at[pl.ds(0, count), pl.ds(0, size)]
+            pltpu.make_async_copy(every, every, dr_sem.at[landing(c)]).wait()
+
+        if ahead and c in (AHEAD, AHEAD + 1):
+            own = (d == 1) if c == AHEAD else (d == 1) & favoured
+            pl.when(own)(lambda: take(deep - 2))
+            pl.when(~own)(lambda: take(deep - 1))
         else:
             take(deep - 1)
 
-    def ahead_rows(other, count=1):
-        size = chunks[AHEAD][1] * share_y
-        return pl.ds(pl.multiple_of(other * size, size), count * size)
-
     def ahead_down():
-        start, size = chunks[AHEAD]
         return pltpu.make_async_remote_copy(
-            src_ref=wa.at[pl.ds(start * north * share_y, size * north * share_y)],
+            src_ref=wa.at[pl.ds(chunks[AHEAD][0] * north * share_y, ein.shape[0])],
             dst_ref=ein,
-            send_sem=ahead_sem.at[2],
+            send_sem=ds_sem.at[0],
             recv_sem=ahead_sem.at[0],
             device_id={"deep": 1},
             device_id_type=pl.DeviceIdType.MESH,
         )
 
-    def ahead_across(target, source):
+    def ahead_block(k, other):
+        first, block = k * north * chunks[AHEAD][1] * share_y, chunks[AHEAD + k][1] * share_y
+        return pl.ds(first + pl.multiple_of(other * block, block), block)
+
+    def ahead_across(k, target, source):
         return pltpu.make_async_remote_copy(
-            src_ref=ein.at[ahead_rows(target)],
-            dst_ref=eu.at[ahead_rows(source)],
-            send_sem=ahead_sem.at[2],
+            src_ref=ein.at[ahead_block(k, target)],
+            dst_ref=eu.at[ahead_block(k, source)],
+            send_sem=ds_sem.at[0],
             recv_sem=ahead_sem.at[1],
             device_id={"north": target},
             device_id_type=pl.DeviceIdType.MESH,
         )
 
-    def ahead_on():
-        return pltpu.make_async_remote_copy(
-            src_ref=ev.at[:, pl.ds(0, part_y)],
-            dst_ref=r.at[2, pl.ds(*chunks[AHEAD])],
+    def ahead_modes(k):
+        (start, size), first = chunks[AHEAD + k], k * chunks[AHEAD][1]
+        for i in range(0, size, 2):
+            pair = min(2, size - i)
+            modes = along_y(eu, k * north * chunks[AHEAD][1] * share_y, size, i, pair, 2 * part_y)
+            for j in range(pair):
+                ev[first + i + j] = modes[:, j * lanes : (j + 1) * lanes]
+        pltpu.make_async_remote_copy(
+            src_ref=ev.at[pl.ds(first, size), pl.ds(0, part_y)],
+            dst_ref=r.at[2, pl.ds(start, size)],
             send_sem=ds_sem.at[0],
-            recv_sem=dr_sem.at[AHEAD],
+            recv_sem=dr_sem.at[landing(AHEAD + k)],
             device_id={"deep": 0},
             device_id_type=pl.DeviceIdType.MESH,
-        )
+        ).start()
+        r[2, pl.ds(start, size)] = ev[pl.ds(first, size), part_y:]
 
     def send_north(picked):
         for c in picked:
@@ -268,8 +284,8 @@
 
     free = max(0, len(chunks) - HELD)
     def send_deep(c):
-        if ahead and c == AHEAD:
-            @pl.when(d != 2)
+        if ahead and c in (AHEAD, AHEAD + 1):
+            @pl.when((d != 2) if c == AHEAD else ((d != 2) | ~favoured))
             def _():
                 for other in (deeps[0], *held):
                     deep_copy(c, other, d).start()
@@ -279,11 +295,14 @@
             far, side = deeps
             deep_copy(c, far, d).start()
             if c < free:
-                if c in NEAR_NOW:
+                if c == free - 1:
+                    @pl.when(~patient)
+                    def _():
+                        deep_copy(c, held[0], d).start()
+                        deep_copy(c, side, d).start()
+                else:
                     deep_copy(c, held[0], d).start()
-                else:
-                    pl.when(~inward)(lambda: deep_copy(c, held[0], d).start())
-                deep_copy(c, side, d).start()
+                    deep_copy(c, side, d).start()
             else:
                 pl.when(inward)(lambda: deep_copy(c, side, d).start())
         else:
@@ -293,7 +312,8 @@
     mine = pl.ds(pl.multiple_of(d * part_y, part_y), part_y)
     tables[0].wait()
     for c in range(len(chunks)):
-        north_landed(c)
+        if c < len(chunks) - 1:
+            north_landed(c)
         if c == 0 and rounds:
             pl.semaphore_wait(round_sem.at[rounds - 1], inner)
         start, size = chunks[c]
@@ -308,10 +328,15 @@
             for late in NEAR_AFTER.get(c, ()):
                 pl.when(inward)(lambda late=late: deep_copy(late, held[0], d).start())
         if last and held:
+            @pl.when(patient)
+            def _():
+                for other in (deeps[1], *held):
+                    deep_copy(free - 1, other, d).start()
+
             @pl.when(~inward)
             def _():
-                for other in (deeps[1], *held):
-                    for late in range(free, len(chunks)):
+                for late in range(free, len(chunks)):
+                    for other in (*held, deeps[1]):
                         deep_copy(late, other, d).start()
         r[d, pl.ds(start, size)] = v[pl.ds(start, size), mine]
         if ahead and c == RELAY:
@@ -319,64 +344,46 @@
             def _():
                 ahead_down().wait_recv()
                 for other in norths:
-                    ahead_across(other, n).start()
-                eu[ahead_rows(n), :] = ein[ahead_rows(n), :]
+                    ahead_across(0, other, n).start()
+                for other in range(few):
+                    @pl.when(n != other)
+                    def _():
+                        ahead_across(1, other, n).start()
+
+                    @pl.when(n == other)
+                    def _():
+                        eu[ahead_block(1, other), :] = ein[ahead_block(1, other), :]
+                eu[ahead_block(0, n), :] = ein[ahead_block(0, n), :]
 
     if ahead:
         @pl.when(d == 1)
         def _():
-            start, size = chunks[AHEAD]
-            every = eu.at[ahead_rows(0, north - 1)]
-            pltpu.make_async_copy(every, every, ahead_sem.at[1]).wait()
-            for i in range(0, size, 2):
-                pair = min(2, size - i)
-                modes = along_y(eu, 0, size, i, pair, 2 * part_y)
-                for k in range(pair):
-                    ev[i + k] = modes[:, k * lanes : (k + 1) * lanes]
-            ahead_on().start()
-            r[2, pl.ds(start, size)] = ev[:, part_y:]
+            def take(size):
+                every = eu.at[pl.ds(0, (north - 1) * size * share_y)]
+                pltpu.make_async_copy(every, every, ahead_sem.at[1]).wait()
+
+            pl.when(favoured)(lambda: take(chunks[AHEAD][1] + chunks[AHEAD + 1][1]))
+            pl.when(~favoured)(lambda: take(chunks[AHEAD][1]))
+            ahead_modes(0)
+            pl.when(favoured)(lambda: ahead_modes(1))
 
     tables[1].wait()
     order = list(range(len(chunks)))
     if ahead:
-        order.remove(AHEAD)
-        order.insert(free - 1, AHEAD)
-    for c in order:
+        order = [RELAY, 0, AHEAD + 1, AHEAD, *range(RELAY + 1, len(chunks))]
+    for c in order[:-1]:
         start, size = chunks[c]
-        deep_landed(c)
+        if not (merged and c == 0):
+            deep_landed(c)
         if held:
             for late in NEAR_THEN.get(c, ()):
                 pl.when(inward)(lambda late=late: deep_copy(late, held[0], d).start())
         parts = [r[s, pl.ds(*chunks[c])].reshape(size * part_y, lanes) for s in range(deep)]
-        factor = fac[pl.ds(start * part_y, size * part_y), :]
-        lines = [
-            jnp.concatenate([p[:, f * share_z : (f + 1) * share_z] for p in parts], axis=1)
-            for f in range(fields)
-        ]
-        if size == 1:
-            count = fields * size * part_y
-            high, low = halves(jnp.concatenate(lines, axis=0))
-            both = jnp.dot(
-                jnp.concatenate([high, low], axis=0),
-                hz[pl.ds(0, grid_z), :],
-                preferred_element_type=jnp.float32,
-            )
-            rest = jnp.dot(high, hz[pl.ds(2 * grid_z, grid_z), :], preferred_element_type=jnp.float32)
-            modes = both[:count] + both[count:] + rest
-            modes = [modes[f * size * part_y : (f + 1) * size * part_y] for f in range(fields)]
-        else:
-            modes = []
-            for f in range(fields):
-                high, low = halves(lines[f])
-                modes.append(
-                    jnp.dot(
-                        jnp.concatenate([high, low, high], axis=1),
-                        hz[...],
-                        preferred_element_type=jnp.float32,
-                    )
-                )
-        for f in range(fields):
-            out[f, pl.ds(*chunks[c])] = (modes[f] * factor).reshape(size, part_y, grid_z)
+        along_z(parts, fac[pl.ds(start * part_y, size * part_y), :], hz, out, start)
+    start, size = chunks[order[-1]]
+    factors[...] = fac[pl.ds(start * part_y, size * part_y), :]
+    deep_landed(order[-1])
+    final[...] = r[:, pl.ds(start, size)]
 
     def sent(semaphore, count):
         every = wa.at[pl.ds(0, count)]
@@ -385,23 +392,63 @@
     across, along = (north - 1) * share_x * share_y, (deep - 1) * share_x * part_y
     sent(ns_sem.at[0], across)
     if ahead:
-        extra = chunks[AHEAD][1]
-
-        @pl.when(d == 1)
-        def _():
-            sent(ahead_sem.at[2], (north - 1) * extra * share_y)
-            sent(ds_sem.at[0], along + extra * part_y)
-
-        @pl.when(d == 2)
-        def _():
-            sent(ahead_sem.at[2], north * extra * share_y)
-            sent(ds_sem.at[0], along - 2 * extra * part_y)
-
-        @pl.when((d == 0) | (d == 3))
-        def _():
-            sent(ds_sem.at[0], along)
+        most, more = chunks[AHEAD][1], chunks[AHEAD + 1][1]
+        for mine, count in ((favoured, more), (~favoured, 0)):
+            down = ein.shape[0] - 2 * (most + count) * part_y
+            over = (north - 1) * most * share_y + (few - (1 if count else 0)) * more * share_y
+            pl.when((d == 1) & mine)(lambda: sent(ds_sem.at[0], along + over + (most + count) * part_y))
+            pl.when((d == 2) & mine)(lambda: sent(ds_sem.at[0], along + down))
+        pl.when(~inward)(lambda: sent(ds_sem.at[0], along))
     else:
         sent(ds_sem.at[0], along)
+
+
+def along_z(parts, factor, hz, out, start):
+    fields, _, part_y, grid_z = out.shape
+    count, share_z = parts[0].shape[0], parts[0].shape[1] // fields
+    size = count // part_y
+    lines = [
+        jnp.concatenate([p[:, f * share_z : (f + 1) * share_z] for p in parts], axis=1) for f in range(fields)
+    ]
+    if size == 1:
+        high, low = halves(jnp.concatenate(lines, axis=0))
+        both = jnp.dot(
+            jnp.concatenate([high, low], axis=0), hz[pl.ds(0, grid_z), :], preferred_element_type=jnp.float32
+        )
+        rest = jnp.dot(high, hz[pl.ds(2 * grid_z, grid_z), :], preferred_element_type=jnp.float32)
+        modes = both[: fields * count] + both[fields * count :] + rest
+        modes = [modes[f * count : (f + 1) * count] for f in range(fields)]
+    else:
+        modes = []
+        for f in range(fields):
+            high, low = halves(lines[f])
+            modes.append(
+                jnp.dot(jnp.concatenate([high, low, high], axis=1), hz[...], preferred_element_type=jnp.float32)
+            )
+    for f in range(fields):
+        out[f, pl.ds(start, size)] = (modes[f] * factor).reshape(size, part_y, grid_z)
+
+
+def finish(done, final, factors, hz, result, rest, sem):
+    fields, share_x = done.shape[:2]
+    deep, size, part_y, lanes = final.shape
+    ahead = share_x - size
+    pieces = sem.shape[1] - 1
+    cuts = [ahead * k // pieces for k in range(pieces + 1)]
+    copies = []
+    for k in range(pieces):
+        for f in range(fields):
+            part = pl.ds(cuts[k], cuts[k + 1] - cuts[k])
+            copies.append(pltpu.make_async_copy(done.at[f, part], result.at[f, part], sem.at[f, k]))
+    for copy in copies:
+        copy.start()
+    parts = [final[s].reshape(size * part_y, lanes) for s in range(deep)]
+    along_z(parts, factors[...], hz, rest, 0)
+    for f in range(fields):
+        copies.append(pltpu.make_async_copy(rest.at[f], result.at[f, pl.ds(ahead, size)], sem.at[f, pieces]))
+        copies[-1].start()
+    for copy in copies:
+        copy.wait()
 
 
 def local(north, deep, forcing, symbol_x, symbol_y, symbol_z):
@@ -427,40 +474,46 @@
     high, low = table_halves(transform_table(grid_z))
     hz = np.concatenate([high, high, low], axis=0)
 
-    groups, extra = 1, chunks[min(AHEAD, len(chunks) - 1)][1]
+    groups, ahead = 1, deep == 4 and len(chunks) > RELAY
+    most, more = (chunks[min(AHEAD + k, len(chunks) - 1)][1] for k in range(2))
     vmem = pl.BlockSpec(memory_space=pltpu.VMEM)
     buffers = [
         pltpu.VMEM((fields, share_y, share_z, grid_x), jnp.float32),
         pltpu.VMEM(hx.shape, jnp.bfloat16),
         pltpu.VMEM(hy.shape, jnp.bfloat16),
-        pltpu.VMEM(hz.shape, jnp.bfloat16),
         pltpu.VMEM((grid_x * share_y, lanes), jnp.float32),
         pltpu.VMEM((grid_y * share_x, lanes), jnp.float32),
         pltpu.VMEM((share_x, grid_y, lanes), jnp.float32),
         pltpu.VMEM((deep, share_x, part_y, lanes), jnp.float32),
         pltpu.VMEM((share_x * part_y, grid_z), jnp.float32),
-        pltpu.VMEM((extra * north * share_y, lanes), jnp.float32),
-        pltpu.VMEM((extra * north * share_y, lanes), jnp.float32),
-        pltpu.VMEM((extra, 2 * part_y, lanes), jnp.float32),
+        pltpu.VMEM(((most * north + more * min(FEW, north)) * share_y, lanes), jnp.float32),
+        pltpu.VMEM(((most + more) * north * share_y, lanes), jnp.float32),
+        pltpu.VMEM((most + more, 2 * part_y, lanes), jnp.float32),
     ]
     result = fields * share_x * part_y * grid_z
     held = sum(math.prod(b.shape) * jnp.dtype(b.dtype).itemsize for b in buffers)
-    return pl.pallas_call(
+    size = chunks[-1][1]
+    done, final, factors, hz = pl.pallas_call(
         functools.partial(kernel, (north, deep, chunks, min(EARLY, len(chunks)))),
-        out_shape=pltpu.VMEM((fields, share_x, part_y, grid_z), jnp.float32),
+        out_shape=[
+            pltpu.VMEM((fields, share_x, part_y, grid_z), jnp.float32),
+            pltpu.VMEM((deep, size, part_y, lanes), jnp.float32),
+            pltpu.VMEM((size * part_y, grid_z), jnp.float32),
+            pltpu.VMEM(hz.shape, jnp.bfloat16),
+        ],
         in_specs=[pl.BlockSpec(memory_space=pltpu.HBM)] * 7,
-        out_specs=vmem,
+        out_specs=[vmem] * 4,
         scratch_shapes=[
             pltpu.VMEM((1, grid_x + grid_y + grid_z), jnp.float32),
             *buffers,
             pltpu.SemaphoreType.DMA((groups,)),
             pltpu.SemaphoreType.DMA((4,)),
             pltpu.SemaphoreType.DMA((1,)),
-            pltpu.SemaphoreType.DMA((len(chunks),)),
+            pltpu.SemaphoreType.DMA((max(1, len(chunks) - 1),)),
             pltpu.SemaphoreType.DMA((1,)),
-            pltpu.SemaphoreType.DMA((len(chunks),)),
+            pltpu.SemaphoreType.DMA((len(chunks) - 1 if ahead else len(chunks),)),
             pltpu.SemaphoreType.REGULAR((max(1, deep - 2),)),
-            pltpu.SemaphoreType.DMA((3,)),
+            pltpu.SemaphoreType.DMA((2,)),
         ],
         compiler_params=pltpu.CompilerParams(
             collective_id=0, has_side_effects=True, vmem_limit_bytes=max(held + 2**23, 60 * 2**20 - 4 * result)
@@ -474,6 +527,17 @@
         symbol_y[None, :],
         symbol_z[None, :],
     )
+    return pl.pallas_call(
+        finish,
+        out_shape=jax.ShapeDtypeStruct((fields, share_x, part_y, grid_z), jnp.float32),
+        in_specs=[vmem] * 4,
+        out_specs=pl.BlockSpec(memory_space=pltpu.HBM),
+        scratch_shapes=[
+            pltpu.VMEM((fields, size, part_y, grid_z), jnp.float32),
+            pltpu.SemaphoreType.DMA((fields, 2)),
+        ],
+        compiler_params=pltpu.CompilerParams(vmem_limit_bytes=2**24),
+    )(*(pltpu.with_memory_space_constraint(held, pltpu.VMEM) for held in (done, final, factors, hz)))
 
 
 def solution(mesh):

time: 32 us -> 31.6 us (0.988)
  local copies, waits for them, and re-layouts: 0.97 us -> 0 us
  Pallas kernels: 30.9 us -> 31.4 us
    pallas_call x0 -> x1, Pallas kernels: none -> 0.99 us  [local(): pl.pallas_call(finish, out_shape=jax.ShapeDtypeStruct((fields, share_x, p...]
    unnamed x1 -> x0, local copies, waits for them, and re-layouts: 0.97 us -> none
    pallas_call x1, Pallas kernels: 30.9 us -> 30.4 us  [local(): pl.pallas_call(functools.partial(kernel, (north, deep, chunks, min(EARLY,...]
where the time goes in v4:
time: 31.6 us; the launch traced here: 31.4 us
  Pallas kernels  31.4 us (99%)
    pallas_call x1, Pallas kernels, local(): pl.pallas_call(functools.partial(kernel, (north, deep, chunks, min(EARLY,...  30.4 us
    pallas_call x1, Pallas kernels, local(): pl.pallas_call(finish, out_shape=jax.ShapeDtypeStruct((fields, share_x, p...  0.99 us

profile of v4, /device:TPU:8, one launch (start us, length us, event | category | flops | bytes accessed | tf_op | source)
XLA Modules:
  0.0 31.4 jit_solution(2007612286984430236)
XLA Ops:
  0.0 30.4 %shard_map.73 = (f32[2,16,32,256]{3,2,1,0:T(8,128)S(1)}, f32[4,1,32,128]{3,2,1,0:T(8,128)S(1)}, f32[32,256]{1,0:T(8,128)S(1)}, bf16[768,256]{1,0:T(8,128)(2,1)S(1)}) custom-call(f32[2,16,64,128]{3,2,1,0:T(8,128)} %bitcast.4, bf16[256,256]{1,0:T(8,128)(2,1)} %constant.6.clone.tx, bf16[128,384]{1,0:T(8,128)(2,1)} %constant.7.clone.ty, ...), custom_call_target="tpu_custom_call" | custom-call | tf_op jit(solution)/shard_map/pallas_call | solution.py:496
  30.4 1.0 %shard_map.74 = f32[2,16,32,256]{3,2,1,0:T(8,128)} custom-call(f32[2,16,32,256]{3,2,1,0:T(8,128)S(1)} %get-tuple-element.9.done, f32[4,1,32,128]{3,2,1,0:T(8,128)S(1)} %get-tuple-element.10.final, f32[32,256]{1,0:T(8,128)S(1)} %get-tuple-element.11.factors, bf16[768,256]{1,0:T(8,128)(2,1)S(1)} %get-tuple-element.12.hz), custom_call_target="tpu_custom_call" | custom-call | tf_op jit(solution)/shard_map/pallas_call | solution.py:530

commit v5 on v4

--- a/solution.py
+++ b/solution.py
@@ -9,7 +9,7 @@
 from jax.experimental.pallas import tpu as pltpu
 from jax.sharding import PartitionSpec as P
 
-CHUNKS = (1, 2, 1, 4, 4, 3, 1)
+CHUNKS = (1, 2, 1, 4, 4, 2, 2)
 EARLY = 3
 HELD = 3
 AHEAD = 1
@@ -410,7 +410,7 @@
     lines = [
         jnp.concatenate([p[:, f * share_z : (f + 1) * share_z] for p in parts], axis=1) for f in range(fields)
     ]
-    if size == 1:
+    if size <= 2:
         high, low = halves(jnp.concatenate(lines, axis=0))
         both = jnp.dot(
             jnp.concatenate([high, low], axis=0), hz[pl.ds(0, grid_z), :], preferred_element_type=jnp.float32

time: 31.6 us -> 31.4 us (level)
  no operation moved by 1% of the time
where the time goes in v5:
time: 31.4 us; the launch traced here: 31.3 us
  Pallas kernels  31.3 us (100%)
    pallas_call x1, Pallas kernels, local(): pl.pallas_call(functools.partial(kernel, (north, deep, chunks, min(EARLY,...  30.3 us
    pallas_call x1, Pallas kernels, local(): pl.pallas_call(finish, out_shape=jax.ShapeDtypeStruct((fields, share_x, p...  0.99 us

profile of v5, /device:TPU:8, one launch (start us, length us, event | category | flops | bytes accessed | tf_op | source)
XLA Modules:
  0.0 31.3 jit_solution(2837711336779724331)
XLA Ops:
  0.0 30.3 %shard_map.73 = (f32[2,16,32,256]{3,2,1,0:T(8,128)S(1)}, f32[4,2,32,128]{3,2,1,0:T(8,128)S(1)}, f32[64,256]{1,0:T(8,128)S(1)}, bf16[768,256]{1,0:T(8,128)(2,1)S(1)}) custom-call(f32[2,16,64,128]{3,2,1,0:T(8,128)} %bitcast.4, bf16[256,256]{1,0:T(8,128)(2,1)} %constant.6.clone.tx, bf16[128,384]{1,0:T(8,128)(2,1)} %constant.7.clone.ty, ...), custom_call_target="tpu_custom_call" | custom-call | tf_op jit(solution)/shard_map/pallas_call | solution.py:496
  30.3 1.0 %shard_map.74 = f32[2,16,32,256]{3,2,1,0:T(8,128)} custom-call(f32[2,16,32,256]{3,2,1,0:T(8,128)S(1)} %get-tuple-element.9.done, f32[4,2,32,128]{3,2,1,0:T(8,128)S(1)} %get-tuple-element.10.final, f32[64,256]{1,0:T(8,128)S(1)} %get-tuple-element.11.factors, bf16[768,256]{1,0:T(8,128)(2,1)S(1)} %get-tuple-element.12.hz), custom_call_target="tpu_custom_call" | custom-call | tf_op jit(solution)/shard_map/pallas_call | solution.py:530

commit v6 on v5

--- a/solution.py
+++ b/solution.py
@@ -13,7 +13,7 @@
 EARLY = 3
 HELD = 3
 AHEAD = 1
-FEW = 2
+OWNERS = (((0, 8),), ((0, 3), (4, 5)))
 RELAY = 3
 NEAR_NOW = (0, 1, 2, 3)
 NEAR_AFTER = {}
@@ -74,11 +74,22 @@
     share_x, part_y = out.shape[1], out.shape[2]
     grid_y, grid_z = v.shape[1], out.shape[3]
     lanes, rounds = fields * share_z, max(0, deep - 2)
-    few = min(FEW, north)
     ahead = merged = deep == 4 and len(chunks) > RELAY
+    if ahead:
+        spans = [[(low, min(high, north)) for low, high in part if low < north] for part in OWNERS]
+        owners = [[other for low, high in part for other in range(low, high)] for part in spans]
+        sent_ahead = sum(len(owners[k]) * chunks[AHEAD + k][1] * share_y for k in range(2))
     n, d = lax.axis_index("north"), lax.axis_index("deep")
     norths, deeps = partners(n, north), partners(d, deep)
-    held, inward, favoured = (), (d == 1) | (d == 2), n < FEW
+    held, inward, favoured = (), (d == 1) | (d == 2), n < 2
+    if ahead:
+        member = [functools.reduce(lambda a, b: a | b, [(n >= low) & (n < high) for low, high in part]) for part in spans]
+        cases = (
+            (member[0] & member[1], (0, 1)),
+            (member[0] & ~member[1], (0,)),
+            (~member[0] & member[1], (1,)),
+            (~member[0] & ~member[1], ()),
+        )
     patient = (d == 3) & favoured
     if deep == 4:
         far = jnp.where(d < 2, 3, 0)
@@ -170,21 +181,30 @@
             pltpu.make_async_copy(every, every, dr_sem.at[landing(c)]).wait()
 
         if ahead and c in (AHEAD, AHEAD + 1):
-            own = (d == 1) if c == AHEAD else (d == 1) & favoured
+            own = (d == 1) & member[c - AHEAD]
             pl.when(own)(lambda: take(deep - 2))
             pl.when(~own)(lambda: take(deep - 1))
         else:
             take(deep - 1)
 
     def ahead_down():
-        return pltpu.make_async_remote_copy(
-            src_ref=wa.at[pl.ds(chunks[AHEAD][0] * north * share_y, ein.shape[0])],
-            dst_ref=ein,
-            send_sem=ds_sem.at[0],
-            recv_sem=ahead_sem.at[0],
-            device_id={"deep": 1},
-            device_id_type=pl.DeviceIdType.MESH,
-        )
+        found = []
+        for k in range(2):
+            start, size = chunks[AHEAD + k]
+            block, base = size * share_y, k * north * chunks[AHEAD][1] * share_y
+            for low, high in spans[k]:
+                part = pl.ds(low * block, (high - low) * block)
+                found.append(
+                    pltpu.make_async_remote_copy(
+                        src_ref=wa.at[pl.ds(start * north * share_y + part.start, part.size)],
+                        dst_ref=ein.at[pl.ds(base + part.start, part.size)],
+                        send_sem=ds_sem.at[0],
+                        recv_sem=ahead_sem.at[0],
+                        device_id={"deep": 1},
+                        device_id_type=pl.DeviceIdType.MESH,
+                    )
+                )
+        return found
 
     def ahead_block(k, other):
         first, block = k * north * chunks[AHEAD][1] * share_y, chunks[AHEAD + k][1] * share_y
@@ -239,7 +259,11 @@
         at += source.shape[1]
     pl.semaphore_wait(barrier, north - 1 + inner)
     if ahead:
-        pl.when(d == 2)(lambda: ahead_down().start())
+        @pl.when(d == 2)
+        def _():
+            for copy in ahead_down():
+                copy.start()
+
     send_north(range(early))
     if rounds:
         signal_beside(round_sem.at[0])
@@ -285,7 +309,7 @@
     free = max(0, len(chunks) - HELD)
     def send_deep(c):
         if ahead and c in (AHEAD, AHEAD + 1):
-            @pl.when((d != 2) if c == AHEAD else ((d != 2) | ~favoured))
+            @pl.when((d != 2) | ~member[c - AHEAD])
             def _():
                 for other in (deeps[0], *held):
                     deep_copy(c, other, d).start()
@@ -342,30 +366,31 @@
         if ahead and c == RELAY:
             @pl.when(d == 1)
             def _():
-                ahead_down().wait_recv()
-                for other in norths:
-                    ahead_across(0, other, n).start()
-                for other in range(few):
-                    @pl.when(n != other)
-                    def _():
-                        ahead_across(1, other, n).start()
-
-                    @pl.when(n == other)
-                    def _():
-                        eu[ahead_block(1, other), :] = ein[ahead_block(1, other), :]
-                eu[ahead_block(0, n), :] = ein[ahead_block(0, n), :]
+                every = ein.at[pl.ds(0, sent_ahead)]
+                pltpu.make_async_copy(every, every, ahead_sem.at[0]).wait()
+                for k in range(2):
+                    for other in owners[k]:
+                        @pl.when(n != other)
+                        def _():
+                            ahead_across(k, other, n).start()
+
+                        @pl.when(n == other)
+                        def _():
+                            eu[ahead_block(k, other), :] = ein[ahead_block(k, other), :]
 
     if ahead:
         @pl.when(d == 1)
         def _():
-            def take(size):
-                every = eu.at[pl.ds(0, (north - 1) * size * share_y)]
-                pltpu.make_async_copy(every, every, ahead_sem.at[1]).wait()
-
-            pl.when(favoured)(lambda: take(chunks[AHEAD][1] + chunks[AHEAD + 1][1]))
-            pl.when(~favoured)(lambda: take(chunks[AHEAD][1]))
-            ahead_modes(0)
-            pl.when(favoured)(lambda: ahead_modes(1))
+            for mine, picked in cases:
+                if picked:
+                    def take():
+                        size = sum(chunks[AHEAD + k][1] for k in picked)
+                        every = eu.at[pl.ds(0, (north - 1) * size * share_y)]
+                        pltpu.make_async_copy(every, every, ahead_sem.at[1]).wait()
+
+                    pl.when(mine)(take)
+            for k in range(2):
+                pl.when(member[k])(lambda: ahead_modes(k))
 
     tables[1].wait()
     order = list(range(len(chunks)))
@@ -392,11 +417,11 @@
     across, along = (north - 1) * share_x * share_y, (deep - 1) * share_x * part_y
     sent(ns_sem.at[0], across)
     if ahead:
-        most, more = chunks[AHEAD][1], chunks[AHEAD + 1][1]
-        for mine, count in ((favoured, more), (~favoured, 0)):
-            down = ein.shape[0] - 2 * (most + count) * part_y
-            over = (north - 1) * most * share_y + (few - (1 if count else 0)) * more * share_y
-            pl.when((d == 1) & mine)(lambda: sent(ds_sem.at[0], along + over + (most + count) * part_y))
+        for mine, picked in cases:
+            own = sum(chunks[AHEAD + k][1] for k in picked)
+            over = sent_ahead - own * share_y + own * part_y
+            down = sent_ahead - 2 * own * part_y
+            pl.when((d == 1) & mine)(lambda: sent(ds_sem.at[0], along + over))
             pl.when((d == 2) & mine)(lambda: sent(ds_sem.at[0], along + down))
         pl.when(~inward)(lambda: sent(ds_sem.at[0], along))
     else:
@@ -433,22 +458,14 @@
     fields, share_x = done.shape[:2]
     deep, size, part_y, lanes = final.shape
     ahead = share_x - size
-    pieces = sem.shape[1] - 1
-    cuts = [ahead * k // pieces for k in range(pieces + 1)]
-    copies = []
-    for k in range(pieces):
-        for f in range(fields):
-            part = pl.ds(cuts[k], cuts[k + 1] - cuts[k])
-            copies.append(pltpu.make_async_copy(done.at[f, part], result.at[f, part], sem.at[f, k]))
-    for copy in copies:
-        copy.start()
+    bulk = pltpu.make_async_copy(done.at[:, pl.ds(0, ahead)], result.at[:, pl.ds(0, ahead)], sem.at[0])
+    bulk.start()
     parts = [final[s].reshape(size * part_y, lanes) for s in range(deep)]
     along_z(parts, factors[...], hz, rest, 0)
-    for f in range(fields):
-        copies.append(pltpu.make_async_copy(rest.at[f], result.at[f, pl.ds(ahead, size)], sem.at[f, pieces]))
-        copies[-1].start()
-    for copy in copies:
-        copy.wait()
+    last = pltpu.make_async_copy(rest, result.at[:, pl.ds(ahead, size)], sem.at[1])
+    last.start()
+    bulk.wait()
+    last.wait()
 
 
 def local(north, deep, forcing, symbol_x, symbol_y, symbol_z):
@@ -486,7 +503,7 @@
         pltpu.VMEM((share_x, grid_y, lanes), jnp.float32),
         pltpu.VMEM((deep, share_x, part_y, lanes), jnp.float32),
         pltpu.VMEM((share_x * part_y, grid_z), jnp.float32),
-        pltpu.VMEM(((most * north + more * min(FEW, north)) * share_y, lanes), jnp.float32),
+        pltpu.VMEM(((most + more) * north * share_y, lanes), jnp.float32),
         pltpu.VMEM(((most + more) * north * share_y, lanes), jnp.float32),
         pltpu.VMEM((most + more, 2 * part_y, lanes), jnp.float32),
     ]
@@ -534,7 +551,7 @@
         out_specs=pl.BlockSpec(memory_space=pltpu.HBM),
         scratch_shapes=[
             pltpu.VMEM((fields, size, part_y, grid_z), jnp.float32),
-            pltpu.SemaphoreType.DMA((fields, 2)),
+            pltpu.SemaphoreType.DMA((2,)),
         ],
         compiler_params=pltpu.CompilerParams(vmem_limit_bytes=2**24),
     )(*(pltpu.with_memory_space_constraint(held, pltpu.VMEM) for held in (done, final, factors, hz)))

time: 31.4 us -> 31.5 us (level)
  no operation moved by 1% of the time
where the time goes in v6:
time: 31.5 us; the launch traced here: 31.3 us
  Pallas kernels  31.3 us (99%)
    pallas_call x1, Pallas kernels, local(): pl.pallas_call(functools.partial(kernel, (north, deep, chunks, min(EARLY,...  30.3 us
    pallas_call x1, Pallas kernels, local(): pl.pallas_call(finish, out_shape=jax.ShapeDtypeStruct((fields, share_x, p...  1 us

profile of v6, /device:TPU:8, one launch (start us, length us, event | category | flops | bytes accessed | tf_op | source)
XLA Modules:
  0.0 31.3 jit_solution(2634968699858326629)
XLA Ops:
  0.0 30.3 %shard_map.73 = (f32[2,16,32,256]{3,2,1,0:T(8,128)S(1)}, f32[4,2,32,128]{3,2,1,0:T(8,128)S(1)}, f32[64,256]{1,0:T(8,128)S(1)}, bf16[768,256]{1,0:T(8,128)(2,1)S(1)}) custom-call(f32[2,16,64,128]{3,2,1,0:T(8,128)} %bitcast.4, bf16[256,256]{1,0:T(8,128)(2,1)} %constant.6.clone.tx, bf16[128,384]{1,0:T(8,128)(2,1)} %constant.7.clone.ty, ...), custom_call_target="tpu_custom_call" | custom-call | tf_op jit(solution)/shard_map/pallas_call | solution.py:513
  30.3 1.0 %shard_map.74 = f32[2,16,32,256]{3,2,1,0:T(8,128)} custom-call(f32[2,16,32,256]{3,2,1,0:T(8,128)S(1)} %get-tuple-element.9.done, f32[4,2,32,128]{3,2,1,0:T(8,128)S(1)} %get-tuple-element.10.final, f32[64,256]{1,0:T(8,128)S(1)} %get-tuple-element.11.factors, bf16[768,256]{1,0:T(8,128)(2,1)S(1)} %get-tuple-element.12.hz), custom_call_target="tpu_custom_call" | custom-call | tf_op jit(solution)/shard_map/pallas_call | solution.py:547

commit v7 on v6

--- a/solution.py
+++ b/solution.py
@@ -13,10 +13,10 @@
 EARLY = 3
 HELD = 3
 AHEAD = 1
-OWNERS = (((0, 8),), ((0, 3), (4, 5)))
+OWNERS = (((0, 8),), ((1, 2), (3, 4), (5, 6), (7, 8)))
 RELAY = 3
 NEAR_NOW = (0, 1, 2, 3)
-NEAR_AFTER = {}
+NEAR_AFTER = {6: (4, 5, 6)}
 NEAR_THEN = {3: (4, 5, 6)}
 
 
@@ -81,6 +81,10 @@
         sent_ahead = sum(len(owners[k]) * chunks[AHEAD + k][1] * share_y for k in range(2))
     n, d = lax.axis_index("north"), lax.axis_index("deep")
     norths, deeps = partners(n, north), partners(d, deep)
+    evens = norths
+    if north % 2 == 0 and north & (north - 1) == 0:
+        chips = partners(n // 2, north // 2)
+        evens = [2 * chip for chip in chips] + [2 * chip + 1 for chip in chips] + norths[-1:]
     held, inward, favoured = (), (d == 1) | (d == 2), n < 2
     if ahead:
         member = [functools.reduce(lambda a, b: a | b, [(n >= low) & (n < high) for low, high in part]) for part in spans]
@@ -239,7 +243,7 @@
 
     def send_north(picked):
         for c in picked:
-            for other in norths:
+            for other in evens if c in (3,) else norths:
                 north_copy(c, other, n).start()
         for c in picked:
             u[rows(c, n), :] = wa[rows(c, n), :]
@@ -350,7 +354,7 @@
         send_deep(c)
         if held:
             for late in NEAR_AFTER.get(c, ()):
-                pl.when(inward)(lambda late=late: deep_copy(late, held[0], d).start())
+                pl.when(inward & ~(n == 0))(lambda late=late: deep_copy(late, held[0], d).start())
         if last and held:
             @pl.when(patient)
             def _():
@@ -402,7 +406,7 @@
             deep_landed(c)
         if held:
             for late in NEAR_THEN.get(c, ()):
-                pl.when(inward)(lambda late=late: deep_copy(late, held[0], d).start())
+                pl.when(inward & (n == 0))(lambda late=late: deep_copy(late, held[0], d).start())
         parts = [r[s, pl.ds(*chunks[c])].reshape(size * part_y, lanes) for s in range(deep)]
         along_z(parts, fac[pl.ds(start * part_y, size * part_y), :], hz, out, start)
     start, size = chunks[order[-1]]

time: 31.5 us -> 31.5 us (level)
  no operation moved by 1% of the time
where the time goes in v7:
time: 31.5 us; the launch traced here: 31.3 us
  Pallas kernels  31.3 us (99%)
    pallas_call x1, Pallas kernels, local(): pl.pallas_call(functools.partial(kernel, (north, deep, chunks, min(EARLY,...  30.3 us
    pallas_call x1, Pallas kernels, local(): pl.pallas_call(finish, out_shape=jax.ShapeDtypeStruct((fields, share_x, p...  1 us

profile of v7, /device:TPU:8, one launch (start us, length us, event | category | flops | bytes accessed | tf_op | source)
XLA Modules:
  0.0 31.3 jit_solution(18355876466079051829)
XLA Ops:
  0.0 30.3 %shard_map.73 = (f32[2,16,32,256]{3,2,1,0:T(8,128)S(1)}, f32[4,2,32,128]{3,2,1,0:T(8,128)S(1)}, f32[64,256]{1,0:T(8,128)S(1)}, bf16[768,256]{1,0:T(8,128)(2,1)S(1)}) custom-call(f32[2,16,64,128]{3,2,1,0:T(8,128)} %bitcast.4, bf16[256,256]{1,0:T(8,128)(2,1)} %constant.6.clone.tx, bf16[128,384]{1,0:T(8,128)(2,1)} %constant.7.clone.ty, ...), custom_call_target="tpu_custom_call" | custom-call | tf_op jit(solution)/shard_map/pallas_call | solution.py:517
  30.3 1.0 %shard_map.74 = f32[2,16,32,256]{3,2,1,0:T(8,128)} custom-call(f32[2,16,32,256]{3,2,1,0:T(8,128)S(1)} %get-tuple-element.9.done, f32[4,2,32,128]{3,2,1,0:T(8,128)S(1)} %get-tuple-element.10.final, f32[64,256]{1,0:T(8,128)S(1)} %get-tuple-element.11.factors, bf16[768,256]{1,0:T(8,128)(2,1)S(1)} %get-tuple-element.12.hz), custom_call_target="tpu_custom_call" | custom-call | tf_op jit(solution)/shard_map/pallas_call | solution.py:551

commit v8 on v7

--- a/solution.py
+++ b/solution.py
@@ -462,13 +462,18 @@
     fields, share_x = done.shape[:2]
     deep, size, part_y, lanes = final.shape
     ahead = share_x - size
-    bulk = pltpu.make_async_copy(done.at[:, pl.ds(0, ahead)], result.at[:, pl.ds(0, ahead)], sem.at[0])
-    bulk.start()
+    bulk = [
+        pltpu.make_async_copy(done.at[f, pl.ds(0, ahead)], result.at[f, pl.ds(0, ahead)], sem.at[f])
+        for f in range(fields)
+    ]
+    for f in range(fields):
+        bulk[f].start(priority=f % 2)
     parts = [final[s].reshape(size * part_y, lanes) for s in range(deep)]
     along_z(parts, factors[...], hz, rest, 0)
-    last = pltpu.make_async_copy(rest, result.at[:, pl.ds(ahead, size)], sem.at[1])
+    last = pltpu.make_async_copy(rest, result.at[:, pl.ds(ahead, size)], sem.at[fields])
     last.start()
-    bulk.wait()
+    for copy in bulk:
+        copy.wait()
     last.wait()
 
 
@@ -555,7 +560,7 @@
         out_specs=pl.BlockSpec(memory_space=pltpu.HBM),
         scratch_shapes=[
             pltpu.VMEM((fields, size, part_y, grid_z), jnp.float32),
-            pltpu.SemaphoreType.DMA((2,)),
+            pltpu.SemaphoreType.DMA((fields + 1,)),
         ],
         compiler_params=pltpu.CompilerParams(vmem_limit_bytes=2**24),
     )(*(pltpu.with_memory_space_constraint(held, pltpu.VMEM) for held in (done, final, factors, hz)))

time: 31.5 us -> 31.5 us (level)
  no operation moved by 1% of the time
where the time goes in v8:
time: 31.5 us; the launch traced here: 31.3 us
  Pallas kernels  31.3 us (99%)
    pallas_call x1, Pallas kernels, local(): pl.pallas_call(functools.partial(kernel, (north, deep, chunks, min(EARLY,...  30.3 us
    pallas_call x1, Pallas kernels, local(): pl.pallas_call(finish, out_shape=jax.ShapeDtypeStruct((fields, share_x, p...  0.99 us

profile of v8, /device:TPU:8, one launch (start us, length us, event | category | flops | bytes accessed | tf_op | source)
XLA Modules:
  0.0 31.3 jit_solution(288199765294534279)
XLA Ops:
  0.0 30.3 %shard_map.73 = (f32[2,16,32,256]{3,2,1,0:T(8,128)S(1)}, f32[4,2,32,128]{3,2,1,0:T(8,128)S(1)}, f32[64,256]{1,0:T(8,128)S(1)}, bf16[768,256]{1,0:T(8,128)(2,1)S(1)}) custom-call(f32[2,16,64,128]{3,2,1,0:T(8,128)} %bitcast.4, bf16[256,256]{1,0:T(8,128)(2,1)} %constant.6.clone.tx, bf16[128,384]{1,0:T(8,128)(2,1)} %constant.7.clone.ty, ...), custom_call_target="tpu_custom_call" | custom-call | tf_op jit(solution)/shard_map/pallas_call | solution.py:522
  30.3 1.0 %shard_map.74 = f32[2,16,32,256]{3,2,1,0:T(8,128)} custom-call(f32[2,16,32,256]{3,2,1,0:T(8,128)S(1)} %get-tuple-element.9.done, f32[4,2,32,128]{3,2,1,0:T(8,128)S(1)} %get-tuple-element.10.final, f32[64,256]{1,0:T(8,128)S(1)} %get-tuple-element.11.factors, bf16[768,256]{1,0:T(8,128)(2,1)S(1)} %get-tuple-element.12.hz), custom_call_target="tpu_custom_call" | custom-call | tf_op jit(solution)/shard_map/pallas_call | solution.py:556
